TPU v7x, 32 devices: a whole 2x2x4 slice. The times are simulated.
32 devices in a mesh: dp: 2 (over core), seq: 8 (over z, y), head: 2 (over x).
Axes of the slice: x: 2, y: 2, z: 4, core: 2. Of those that a mesh axis runs over, the one named last changes fastest.
Arguments:
- hidden_in: bfloat16 [8, 1024, 1536], P('dp', 'seq'), may hold values from -6 to 6
- segment_ids: int32 [8, 1024], P('dp', 'seq'), may hold values from 0 to 6, as said below
- position_ids: int32 [8, 1024], P('dp', 'seq'), may hold values from 0 to 1017, as said below
- out_cot: bfloat16 [8, 1024, 1536], P('dp', 'seq'), may hold values from -6 to 6
- attn_gain: bfloat16 [1536], replicated, may hold values from 0.5 to 1.5
- w_query: bfloat16 [1536, 1536], P(('dp', 'seq'), 'head'), may hold values from -0.15625 to 0.15625
- b_query: bfloat16 [12, 128], P('head'), may hold values from -3 to 3
- w_key: bfloat16 [1536, 256], P(('dp', 'seq'), 'head'), may hold values from -0.15625 to 0.15625
- b_key: bfloat16 [2, 128], P('head'), may hold values from -3 to 3
- w_value: bfloat16 [1536, 256], P(('dp', 'seq'), 'head'), may hold values from -0.15625 to 0.15625
- b_value: bfloat16 [2, 128], P('head'), may hold values from -3 to 3
- w_out: bfloat16 [1536, 1536], P('head', ('dp', 'seq')), may hold values from -0.625 to 0.625
- ffn_gain: bfloat16 [1536], replicated, may hold values from 0.5 to 1.5
- w_gate: bfloat16 [1536, 8960], P(('dp', 'seq'), 'head'), may hold values from -0.15625 to 0.15625
- w_up: bfloat16 [1536, 8960], P(('dp', 'seq'), 'head'), may hold values from -0.15625 to 0.15625
- w_down: bfloat16 [8960, 1536], P('head', ('dp', 'seq')), may hold values from -0.125 to 0.125
Outputs:
- layer_out: bfloat16 [8, 1024, 1536], P('dp', 'seq')
- input_grad: bfloat16 [8, 1024, 1536], P('dp', 'seq')
- grad_attn_gain: float32 [1536], P(('dp', 'seq'))
- grad_w_query: float32 [1536, 1536], P(('dp', 'seq'), 'head')
- grad_b_query: float32 [12, 128], P('head', ('dp', 'seq'))
- grad_w_key: float32 [1536, 256], P(('dp', 'seq'), 'head')
- grad_b_key: float32 [2, 128], P('head')
- grad_w_value: float32 [1536, 256], P(('dp', 'seq'), 'head')
- grad_b_value: float32 [2, 128], P('head', ('dp', 'seq'))
- grad_w_out: float32 [1536, 1536], P('head', ('dp', 'seq'))
- grad_ffn_gain: float32 [1536], P(('dp', 'seq'))
- grad_w_gate: float32 [1536, 8960], P(('dp', 'seq'), 'head')
- grad_w_up: float32 [1536, 8960], P(('dp', 'seq'), 'head')
- grad_w_down: float32 [8960, 1536], P('head', ('dp', 'seq'))
Inputs may be any that keep to these rules, and one draw needn't show every extreme that they name: `segment_ids`: each row's 1024 positions are stored in blocks of 128: block number b holds the row's natural positions b * 64 to b * 64 + 63, then 1024 - (b + 1) * 64 to 1024 - b * 64 - 1, each in rising order. In natural order a row holds 6 documents of uneven lengths with ids 1 to 6, rising, then one or more padding positions with id 0. `position_ids`: in natural order (stored as for segment_ids) the ids count 0, 1, 2 and so on from the start of each document and of the padding.
All inputs are finite; a program needn't handle non-finite values.
Results may differ from a plain program's by a relative error of at most 0.024.
Values may be sent and summed in bfloat16 or wider, within the bound.
A program may use at most 256 MiB of HBM per device.

v0:
```python
import math
import jax
import jax.numpy as jnp
from jax import lax
from jax.sharding import PartitionSpec as P

EPSILON = 1e-06
THETA = 1000000.0
MASKED = -1e30


def rope_tables(position, head_size):
    half_size = head_size // 2
    frequency = THETA ** (-jnp.arange(half_size, dtype=jnp.float32) * 2.0 / head_size)
    angles = position.astype(jnp.float32)[:, None] * frequency[None, :]
    return (jnp.cos(angles)[:, None, :], jnp.sin(angles)[:, None, :])


def rotate(values, cosine, sine_table, direction):
    half_size = values.shape[-1] // 2
    first_half = values[..., :half_size]
    second_half = values[..., half_size:]
    return jnp.concatenate(
        [
            first_half * cosine - direction * (second_half * sine_table),
            second_half * cosine + direction * (first_half * sine_table),
        ],
        axis=-1,
    )


def plain_dot(left, right):
    return jnp.dot(left, right, preferred_element_type=jnp.float32)


def grad_of_weight(left, right):
    return lax.dot_general(
        left, right, (((0,), (0,)), ((), ())), preferred_element_type=jnp.float32
    )


def through_weight(left, right):
    return lax.dot_general(
        left, right, (((1,), (1,)), ((), ())), preferred_element_type=jnp.float32
    )


def norm_scale(values):
    return lax.rsqrt(jnp.mean(values * values, axis=-1, keepdims=True) + EPSILON)


def norm_back(grad_in, values, scale_rows, gain):
    scaled = grad_in * gain
    cubed = scale_rows * scale_rows * scale_rows
    return scale_rows * scaled - values * cubed * jnp.mean(scaled * values, axis=-1, keepdims=True)


def block_scores(queries, key_block, key_marks, own_marks, factor):
    scores = (
        jnp.einsum("rqgd,rtd->rgqt", queries, key_block, preferred_element_type=jnp.float32)
        * factor
    )
    allowed = (own_marks[0][:, :, None] == key_marks[0][:, None, :]) & (
        key_marks[1][:, None, :] <= own_marks[1][:, :, None]
    )
    return (scores, allowed[:, None, :, :])


def on_device(
    hidden_in,
    segment_ids,
    position_ids,
    out_cot,
    attn_gain,
    w_query,
    b_query,
    w_key,
    b_key,
    w_value,
    b_value,
    w_out,
    ffn_gain,
    w_gate,
    w_up,
    w_down,
):
    row_count, row_width, model_width = hidden_in.shape
    tokens = row_count * row_width
    groups, head_size = b_query.shape
    factor = head_size ** (-0.5)
    full_query, full_key, full_value, full_gate, full_up, full_out, full_down = (
        lax.all_gather(w_query, ("dp", "seq"), axis=0, tiled=True),
        lax.all_gather(w_key, ("dp", "seq"), axis=0, tiled=True),
        lax.all_gather(w_value, ("dp", "seq"), axis=0, tiled=True),
        lax.all_gather(w_gate, ("dp", "seq"), axis=0, tiled=True),
        lax.all_gather(w_up, ("dp", "seq"), axis=0, tiled=True),
        lax.all_gather(w_out, ("dp", "seq"), axis=1, tiled=True),
        lax.all_gather(w_down, ("dp", "seq"), axis=1, tiled=True),
    )
    own_marks = jnp.stack([segment_ids, position_ids])
    key_labels = lax.all_gather(own_marks, "seq", axis=2, tiled=True)
    length = key_labels.shape[2]
    key_rows = math.gcd(length, 512)
    block_count = length // key_rows
    hidden = hidden_in.reshape(tokens, model_width).astype(jnp.float32)
    scale_one = norm_scale(hidden)
    gain_one = attn_gain.astype(jnp.float32)
    normed = (hidden * scale_one * gain_one).astype(jnp.bfloat16)
    cosine, sine_table = rope_tables(position_ids.reshape(tokens), head_size)
    query_pre = plain_dot(normed, full_query) + b_query.reshape(-1).astype(jnp.float32)
    key_pre = plain_dot(normed, full_key) + b_key.reshape(-1).astype(jnp.float32)
    value_pre = plain_dot(normed, full_value) + b_value.reshape(-1).astype(jnp.float32)
    queries = rotate(query_pre.reshape(tokens, groups, head_size), cosine, sine_table, 1.0).astype(
        jnp.bfloat16
    )
    queries = queries.reshape(row_count, row_width, groups, head_size)
    key_rot = rotate(key_pre.reshape(tokens, 1, head_size), cosine, sine_table, 1.0).astype(
        jnp.bfloat16
    )
    local_kv = jnp.concatenate(
        [key_rot.reshape(tokens, head_size), value_pre.astype(jnp.bfloat16)], axis=-1
    )
    all_kv = lax.all_gather(
        local_kv.reshape(row_count, row_width, 2 * head_size), "seq", axis=1, tiled=True
    )

    def key_slices(step_index):
        offset = step_index * key_rows
        kv_block = lax.dynamic_slice_in_dim(all_kv, offset, key_rows, 1)
        key_marks = lax.dynamic_slice_in_dim(key_labels, offset, key_rows, 2)
        scores, allowed = block_scores(
            queries, kv_block[..., :head_size], key_marks, own_marks, factor
        )
        return (offset, kv_block, scores, allowed)

    def max_step(step_index, state_pair):
        running_max, running_sum = state_pair
        offset, kv_block, scores, allowed = key_slices(step_index)
        masked = jnp.where(allowed, scores, MASKED)
        fresh_max = jnp.maximum(running_max, jnp.max(masked, axis=-1))
        exp_terms = jnp.where(allowed, jnp.exp(masked - fresh_max[..., None]), 0.0)
        return (
            fresh_max,
            running_sum * jnp.exp(running_max - fresh_max) + jnp.sum(exp_terms, axis=-1),
        )

    stat_shape = (row_count, groups, row_width)
    running_max, running_sum = lax.fori_loop(
        0,
        block_count,
        max_step,
        (jnp.full(stat_shape, MASKED, jnp.float32), jnp.zeros(stat_shape, jnp.float32)),
    )
    log_total = running_max + jnp.log(running_sum)

    def block_probs(scores, allowed):
        return jnp.where(allowed, jnp.exp(scores - log_total[..., None]), 0.0)

    def output_step(step_index, accum):
        offset, kv_block, scores, allowed = key_slices(step_index)
        weights = block_probs(scores, allowed).astype(jnp.bfloat16)
        return accum + jnp.einsum(
            "rgqt,rtd->rqgd", weights, kv_block[..., head_size:], preferred_element_type=jnp.float32
        )

    attended = lax.fori_loop(
        0,
        block_count,
        output_step,
        jnp.zeros((row_count, row_width, groups, head_size), jnp.float32),
    )
    mixed = attended.reshape(tokens, groups * head_size).astype(jnp.bfloat16)
    middle = hidden + lax.psum(plain_dot(mixed, full_out), "head")
    scale_two = norm_scale(middle)
    gain_two = ffn_gain.astype(jnp.float32)
    normed_two = (middle * scale_two * gain_two).astype(jnp.bfloat16)
    gate_pre = plain_dot(normed_two, full_gate)
    up_pre = plain_dot(normed_two, full_up)
    sigmoid_gate = jax.nn.sigmoid(gate_pre)
    activated = gate_pre * sigmoid_gate
    product = (activated * up_pre).astype(jnp.bfloat16)
    result = middle + lax.psum(plain_dot(product, full_down).astype(jnp.bfloat16), "head").astype(
        jnp.float32
    )
    layer_out = result.astype(jnp.bfloat16).reshape(row_count, row_width, model_width)
    live_rows = (segment_ids != 0).astype(jnp.float32).reshape(tokens, 1)
    cotangent = out_cot.reshape(tokens, model_width).astype(jnp.float32) * live_rows
    cot_low = cotangent.astype(jnp.bfloat16)
    full_query, full_key, full_value, full_gate, full_up, full_out, full_down = (
        lax.all_gather(w_query, ("dp", "seq"), axis=0, tiled=True),
        lax.all_gather(w_key, ("dp", "seq"), axis=0, tiled=True),
        lax.all_gather(w_value, ("dp", "seq"), axis=0, tiled=True),
        lax.all_gather(w_gate, ("dp", "seq"), axis=0, tiled=True),
        lax.all_gather(w_up, ("dp", "seq"), axis=0, tiled=True),
        lax.all_gather(w_out, ("dp", "seq"), axis=1, tiled=True),
        lax.all_gather(w_down, ("dp", "seq"), axis=1, tiled=True),
    )
    grad_down_w = grad_of_weight(product, cot_low)
    d_product = through_weight(cot_low, full_down).astype(jnp.bfloat16).astype(jnp.float32)
    d_gate = (d_product * up_pre * sigmoid_gate * (1.0 + gate_pre * (1.0 - sigmoid_gate))).astype(
        jnp.bfloat16
    )
    d_up = (d_product * activated).astype(jnp.bfloat16)
    grad_gate_w = grad_of_weight(normed_two, d_gate)
    grad_up_w = grad_of_weight(normed_two, d_up)
    back_two = lax.psum(through_weight(d_gate, full_gate) + through_weight(d_up, full_up), "head")
    gain_two_grad = jnp.sum(back_two * middle * scale_two, axis=0)
    gate_sum, up_sum, down_sum, gain_two_sum = (grad_gate_w, grad_up_w, grad_down_w, gain_two_grad)
    d_middle = cotangent + norm_back(back_two, middle, scale_two, gain_two)
    d_middle_low = d_middle.astype(jnp.bfloat16)
    grad_out_w = grad_of_weight(mixed, d_middle_low)
    d_mixed = (
        through_weight(d_middle_low, full_out)
        .astype(jnp.bfloat16)
        .reshape(row_count, row_width, groups, head_size)
    )

    def delta_step(step_index, row_delta):
        offset, kv_block, scores, allowed = key_slices(step_index)
        probs = block_probs(scores, allowed)
        d_probs = jnp.einsum(
            "rqgd,rtd->rgqt", d_mixed, kv_block[..., head_size:], preferred_element_type=jnp.float32
        )
        return row_delta + jnp.sum(probs * d_probs, axis=-1)

    row_delta = lax.fori_loop(0, block_count, delta_step, jnp.zeros(stat_shape, jnp.float32))

    def grad_step(step_index, state_pair):
        query_accum, kv_buffer = state_pair
        offset, kv_block, scores, allowed = key_slices(step_index)
        probs = block_probs(scores, allowed)
        weights = probs.astype(jnp.bfloat16)
        d_probs = jnp.einsum(
            "rqgd,rtd->rgqt", d_mixed, kv_block[..., head_size:], preferred_element_type=jnp.float32
        )
        d_scores = (probs * (d_probs - row_delta[..., None])).astype(jnp.bfloat16)
        query_accum = query_accum + jnp.einsum(
            "rgqt,rtd->rqgd",
            d_scores,
            kv_block[..., :head_size],
            preferred_element_type=jnp.float32,
        )
        key_terms = jnp.einsum(
            "rgqt,rqgd->rtd", d_scores, queries, preferred_element_type=jnp.float32
        )
        value_terms = jnp.einsum(
            "rgqt,rqgd->rtd", weights, d_mixed, preferred_element_type=jnp.float32
        )
        kv_buffer = lax.dynamic_update_slice_in_dim(
            kv_buffer, jnp.concatenate([key_terms, value_terms], axis=-1), offset, 1
        )
        return (query_accum, kv_buffer)

    query_accum, kv_buffer = lax.fori_loop(
        0,
        block_count,
        grad_step,
        (
            jnp.zeros((row_count, row_width, groups, head_size), jnp.float32),
            jnp.zeros((row_count, length, 2 * head_size), jnp.float32),
        ),
    )
    d_kv = lax.psum_scatter(kv_buffer, "seq", scatter_dimension=1, tiled=True).reshape(
        tokens, 2 * head_size
    )
    d_key = (
        rotate(
            (d_kv[:, :head_size] * factor).reshape(tokens, 1, head_size), cosine, sine_table, -1.0
        )
        .reshape(tokens, head_size)
        .astype(jnp.bfloat16)
    )
    d_value = d_kv[:, head_size:].astype(jnp.bfloat16)
    d_query = (
        rotate(query_accum.reshape(tokens, groups, head_size) * factor, cosine, sine_table, -1.0)
        .reshape(tokens, groups * head_size)
        .astype(jnp.bfloat16)
    )
    replicas = lax.axis_size(("dp", "seq"))
    bias_query = jnp.sum(d_query.astype(jnp.float32), axis=0).reshape(groups, head_size)
    bias_key = jnp.sum(d_key.astype(jnp.float32), axis=0).reshape(1, head_size)
    bias_key_wide = jnp.tile(bias_key, (1, replicas))
    bias_value = jnp.sum(d_value.astype(jnp.float32), axis=0).reshape(1, head_size)
    grad_query_w = grad_of_weight(normed, d_query)
    grad_key_w = grad_of_weight(normed, d_key)
    grad_value_w = grad_of_weight(normed, d_value)
    back_one = (
        through_weight(d_query, full_query)
        + through_weight(d_key, full_key)
        + through_weight(d_value, full_value)
    )
    back_one = lax.psum(back_one.astype(jnp.bfloat16), "head").astype(jnp.float32)
    gain_one_grad = jnp.sum(back_one * hidden * scale_one, axis=0)
    d_hidden = d_middle + norm_back(back_one, hidden, scale_one, gain_one)
    input_grad = d_hidden.astype(jnp.bfloat16).reshape(row_count, row_width, model_width)
    (
        query_sum,
        key_sum,
        value_sum,
        out_sum,
        gain_one_sum,
        bq_sum,
        bk_sum,
        bv_sum,
        gate_sum,
        up_sum,
        down_sum,
        gain_two_sum,
    ) = (
        lax.psum_scatter(grad_query_w, ("dp", "seq"), scatter_dimension=0, tiled=True),
        lax.psum_scatter(grad_key_w, ("dp", "seq"), scatter_dimension=0, tiled=True),
        lax.psum_scatter(grad_value_w, ("dp", "seq"), scatter_dimension=0, tiled=True),
        lax.psum_scatter(grad_out_w, ("dp", "seq"), scatter_dimension=1, tiled=True),
        lax.psum_scatter(gain_one_grad, ("dp", "seq"), scatter_dimension=0, tiled=True),
        lax.psum_scatter(bias_query, ("dp", "seq"), scatter_dimension=1, tiled=True),
        lax.psum_scatter(bias_key_wide, ("dp", "seq"), scatter_dimension=1, tiled=True),
        lax.psum_scatter(bias_value, ("dp", "seq"), scatter_dimension=1, tiled=True),
        lax.psum_scatter(gate_sum, ("dp", "seq"), scatter_dimension=0, tiled=True),
        lax.psum_scatter(up_sum, ("dp", "seq"), scatter_dimension=0, tiled=True),
        lax.psum_scatter(down_sum, ("dp", "seq"), scatter_dimension=1, tiled=True),
        lax.psum_scatter(gain_two_sum, ("dp", "seq"), scatter_dimension=0, tiled=True),
    )
    return (
        layer_out,
        input_grad,
        gain_one_sum,
        query_sum,
        bq_sum,
        key_sum,
        bk_sum,
        value_sum,
        bv_sum,
        out_sum,
        gain_two_sum,
        gate_sum,
        up_sum,
        down_sum,
    )


def solution(mesh):
    placed = (
        P("dp", "seq", None),
        P("dp", "seq"),
        P("dp", "seq"),
        P("dp", "seq", None),
        P(),
        P(("dp", "seq"), "head"),
        P("head", None),
        P(("dp", "seq"), "head"),
        P("head", None),
        P(("dp", "seq"), "head"),
        P("head", None),
        P("head", ("dp", "seq")),
        P(),
        P(("dp", "seq"), "head"),
        P(("dp", "seq"), "head"),
        P("head", ("dp", "seq")),
    )
    return jax.shard_map(
        on_device,
        mesh=mesh,
        in_specs=placed,
        out_specs=(
            P("dp", "seq", None),
            P("dp", "seq", None),
            P(("dp", "seq")),
            P(("dp", "seq"), "head"),
            P("head", ("dp", "seq")),
            P(("dp", "seq"), "head"),
            P("head", None),
            P(("dp", "seq"), "head"),
            P("head", ("dp", "seq")),
            P("head", ("dp", "seq")),
            P(("dp", "seq")),
            P(("dp", "seq"), "head"),
            P(("dp", "seq"), "head"),
            P("head", ("dp", "seq")),
        ),
        check_vma=False,
    )
```

profile of v0, /device:TPU:0, one launch (start us, length us, event | category | flops | bytes accessed | tf_op | source)
XLA Modules:
  0.0 2139.3 jit_solution(3503738205872189389)
XLA Ops:
  8.7 38.7 %all_gather.34 = bf16[1536,128]{1,0:T(8,128)(2,1)S(1)} all-gather(bf16[96,128]{1,0:T(8,128)(2,1)} %param.31), channel_id=1, replica_groups=mesh['dp'=2,'seq'=8,'head'=2] {'dp','seq'}, dimensions={0}, use_global_device_ids=true | all-gather | bytes 417792 | tf_op jit(solution)/shard_map/all_gather | solution.py:93
  53.2 30.5 %all_gather.35 = bf16[1536,128]{1,0:T(8,128)(2,1)S(1)} all-gather(bf16[96,128]{1,0:T(8,128)(2,1)S(1)} %copy-done.46), channel_id=1, replica_groups=mesh['dp'=2,'seq'=8,'head'=2] {'dp','seq'}, dimensions={0}, use_global_device_ids=true | all-gather | bytes 417792 | tf_op jit(solution)/shard_map/all_gather | solution.py:94
  88.3 26.5 %all_gather.37 = s32[2,4,1024]{2,1,0:T(4,128)S(1)} all-gather(s32[2,4,128]{2,1,0:T(4,128)S(1)} %pad_add_fusion), channel_id=1, replica_groups=mesh['dp'=2,'seq'=8,'head'=2] {'seq'}, dimensions={2}, use_global_device_ids=true | all-gather | bytes 36864 | tf_op jit(solution)/shard_map/all_gather | solution.py:101
  125.2 10.0 all-gather.7.cloned.1.call-done
  135.3 19.7 while.60
  155.0 10.3 while.61
  167.5 10.9 all-gather.11.cloned.1.call-done
  188.1 79.8 %all-reduce.10.cloned.1.call-done = f32[512,1536]{1,0:T(8,128)} async-done(((f32[512,1536]{1,0:T(8,128)}), f32[512,1536]{1,0:T(8,128)}) %all-reduce.10.cloned.1.call-update) | async-done | bytes 3145744 | tf_op jit(solution)/shard_map/psum | solution.py:173
  273.4 104.3 %all-gather.17.cloned.1.call-done = bf16[4480,1536]{0,1:T(8,128)(2,1)} async-done(((bf16[4480,96]{0,1:T(8,128)(2,1)}), bf16[4480,1536]{0,1:T(8,128)(2,1)}) %all-gather.17.cloned.1.call-update) | async-done | bytes 13762576 | tf_op jit(solution)/shard_map/all_gather | solution.py:98
  377.7 14.3 convolution_convert_fusion
  392.0 93.7 %all-gather.13.cloned.1.call-done = bf16[1536,4480]{1,0:T(8,128)(2,1)} async-done(((bf16[96,4480]{1,0:T(8,128)(2,1)}), bf16[1536,4480]{1,0:T(8,128)(2,1)}) %all-gather.13.cloned.1.call-update) | async-done | bytes 13762576 | tf_op jit(solution)/shard_map/all_gather | solution.py:95
  485.7 13.2 fusion.107
  498.8 95.0 %all-gather.15.cloned.1.call-done = bf16[1536,4480]{1,0:T(8,128)(2,1)} async-done(((bf16[96,4480]{1,0:T(8,128)(2,1)}), bf16[1536,4480]{1,0:T(8,128)(2,1)}) %all-gather.15.cloned.1.call-update) | async-done | bytes 13762576 | tf_op jit(solution)/shard_map/all_gather | solution.py:96
  593.8 17.7 fusion.46
  613.6 12.0 fusion.108
  625.6 19.2 convolution_add_fusion.2
  646.4 82.6 %all-reduce.12.cloned.1.call-done = f32[512,1536]{1,0:T(8,128)} async-done(((f32[512,1536]{1,0:T(8,128)}), f32[512,1536]{1,0:T(8,128)}) %all-reduce.12.cloned.1.call-update) | async-done | bytes 3145744 | tf_op jit(solution)/shard_map/psum | solution.py:206
  740.1 20.2 while.62
  762.7 43.6 %while.63 = (s32[]{:T(128)}, f32[4,128,6,128]{1,3,2,0:T(8,128)}, f32[4,1024,256]{1,2,0:T(8,128)}, bf16[4,1024,256]{2,1,0:T(8,128)(2,1)}, s32[4,128]{1,0:T(4,128)...) while((s32[]{:T(128)}, f32[4,128,6,128]{1,3,2,0:T(8,128)}, ...), condition=%wide.region_16.17_spmd.clone, body=%wide.region_15.16_spmd.clone.sunk | while | flops 2031091712 | bytes 111866424 | solution.py:254
  806.4 13.2 convolution_convert_fusion.1
  827.7 67.5 %reduce-scatter.14.cloned.1.call-done = f32[4,128,256]{1,2,0:T(8,128)} async-done(((f32[4,1024,256]{1,2,0:T(8,128)}), f32[4,128,256]{1,2,0:T(8,128)}) %reduce-scatter.14.cloned.1.call-update) | async-done | bytes 524304 | tf_op jit(solution)/shard_map/reduce_scatter | solution.py:263
  924.3 15.1 fusion.111
  939.5 18.1 fusion.103
  959.0 15.1 fusion.112
  978.1 69.3 %all-reduce.14.cloned.1.call-done = (bf16[512,1536]{1,0:T(8,128)(2,1)}, bf16[512,1536]{1,0:T(8,128)(2,1)}) async-done(((bf16[512,1536]{1,0:T(8,128)(2,1)}, bf16[512,1536]{1,0:T(8,128)(2,1)}), (bf16[512,1536]{1,0:T(8,128)(2,1)}, bf16[512,1536]{1,0:T(8,128)(2,1)})) %all-reduce.14.cloned.1.call-update) | async-done | bytes 3145744 | tf_op jit(solution)/shard_map/psum | solution.py:182
  1050.6 62.7 %all-reduce.4 = (f32[1536]{0:T(1024)S(1)}, f32[6,128]{1,0:T(8,128)S(1)}, f32[1,128]{1,0:T(1,128)S(1)}, f32[1536]{0:T(1024)S(1)}) all-reduce(f32[1536]{0:T(1024)S(1)} %get-tuple-element.868, f32[6,128]{1,0:T(8,128)S(1)} %get-tuple-element.948, ...), channel_id=3, replica_groups=mesh['dp'=2,'seq'=8,'head'=2] {'dp','seq'}, use_global_device_ids=true, to_apply=%region_21.22.clone | all-reduce | flops 3968 | bytes 31744
  1128.1 79.2 %reduce-scatter.22.cloned.1.call-done = f32[768,96]{0,1:T(8,128)} async-done(((f32[768,1536]{0,1:T(8,128)}), f32[768,96]{0,1:T(8,128)}) %reduce-scatter.22.cloned.1.call-update) | async-done | bytes 294928 | tf_op jit(solution)/shard_map/reduce_scatter | solution.py:313
  1207.3 59.9 %reduce-scatter.18.cloned.1.call-done = f32[96,128]{1,0:T(8,128)} async-done(((f32[1536,128]{1,0:T(8,128)}), f32[96,128]{1,0:T(8,128)}) %reduce-scatter.18.cloned.1.call-update) | async-done | bytes 49168 | tf_op jit(solution)/shard_map/reduce_scatter | solution.py:311
  1267.2 59.8 %reduce-scatter.20.cloned.1.call-done = f32[96,128]{1,0:T(8,128)} async-done(((f32[1536,128]{1,0:T(8,128)}), f32[96,128]{1,0:T(8,128)}) %reduce-scatter.20.cloned.1.call-update) | async-done | bytes 49168 | tf_op jit(solution)/shard_map/reduce_scatter | solution.py:312
  1327.0 268.3 %reduce-scatter.24.cloned.1.call-done = f32[96,4480]{1,0:T(8,128)} async-done(((f32[1536,4480]{1,0:T(8,128)}), f32[96,4480]{1,0:T(8,128)}) %reduce-scatter.24.cloned.1.call-update) | async-done | bytes 1720336 | tf_op jit(solution)/shard_map/reduce_scatter | solution.py:318
  1595.2 268.4 %reduce-scatter.26.cloned.1.call-done = f32[96,4480]{1,0:T(8,128)} async-done(((f32[1536,4480]{1,0:T(8,128)}), f32[96,4480]{1,0:T(8,128)}) %reduce-scatter.26.cloned.1.call-update) | async-done | bytes 1720336 | tf_op jit(solution)/shard_map/reduce_scatter | solution.py:319
  1863.6 268.4 %reduce-scatter.28.cloned.1.call-done = f32[4480,96]{0,1:T(8,128)} async-done(((f32[4480,1536]{0,1:T(8,128)}), f32[4480,96]{0,1:T(8,128)}) %reduce-scatter.28.cloned.1.call-update) | async-done | bytes 1720336 | tf_op jit(solution)/shard_map/reduce_scatter | solution.py:320
  (308 shorter events, 208.5 us)
Async XLA Ops:
  7.2 43.4 %copy-start.7 = (bf16[4,128,1536]{2,1,0:T(8,128)(2,1)S(1)}, bf16[4,128,1536]{2,1,0:T(8,128)(2,1)}, u32[]{:S(2)}) copy-start(bf16[4,128,1536]{2,1,0:T(8,128)(2,1)} %param.24) | copy-start | bytes 4718596
  7.2 107.6 %all-gather.9.cloned.1.call-start = ((), (), s32[]{:S(2)}) async-start(), calls=%async_computation.10 | async-start | bytes 2506752 | tf_op jit(solution)/shard_map/all_gather | solution.py:92
  7.9 127.3 %all-gather.7.cloned.1.call-start = ((), (), s32[]{:S(2)}) async-start(), calls=%async_computation.9 | async-start | bytes 2359296 | tf_op jit(solution)/shard_map/all_gather | solution.py:123
  8.7 43.1 %copy-start.39 = (f32[1536]{0:T(1024)}, f32[1536]{0:T(1024)S(1)}, u32[]{:S(2)}) copy-start(f32[1536]{0:T(1024)S(1)} %convert_element_type.175) | copy-start | bytes 18436
  8.7 79.0 %copy-start.52 = (f32[64]{0:T(128)}, f32[64]{0:T(128)S(1)}, u32[]{:S(2)}) copy-start(f32[64]{0:T(128)S(1)} %multiply_power_fusion) | copy-start | bytes 772
  51.0 63.8 %copy-start.11 = (bf16[512,1536]{1,0:T(8,128)(2,1)}, bf16[512,1536]{1,0:T(8,128)(2,1)S(1)}, u32[]{:S(2)}) copy-start(bf16[512,1536]{1,0:T(8,128)(2,1)S(1)} %fusion.63) | copy-start | bytes 4718596
  51.0 63.7 %copy-start.55 = (bf16[6,128]{1,0:T(8,128)(2,1)S(1)}, bf16[6,128]{1,0:T(8,128)(2,1)}, u32[]{:S(2)}) copy-start(bf16[6,128]{1,0:T(8,128)(2,1)} %param.30) | copy-start | bytes 4612
  86.8 91.5 %all-gather.11.cloned.1.call-start = ((), (), s32[]{:S(2)}) async-start(), calls=%async_computation.11 | async-start | bytes 2506752 | tf_op jit(solution)/shard_map/all_gather | solution.py:97
  87.6 180.3 %all-reduce.10.cloned.1.call-start = ((), (), s32[]{:S(2)}) async-start(), calls=%async_computation.12 | async-start | bytes 6291456 | tf_op jit(solution)/shard_map/psum | solution.py:173
  183.2 194.5 %all-gather.17.cloned.1.call-start = ((), (), s32[]{:S(2)}) async-start(), calls=%async_computation.15 | async-start | bytes 14622720 | tf_op jit(solution)/shard_map/all_gather | solution.py:98
  183.8 301.9 %all-gather.13.cloned.1.call-start = ((), (), s32[]{:S(2)}) async-start(), calls=%async_computation.13 | async-start | bytes 14622720 | tf_op jit(solution)/shard_map/all_gather | solution.py:95
  184.4 409.5 %all-gather.15.cloned.1.call-start = ((), (), s32[]{:S(2)}) async-start(), calls=%async_computation.14 | async-start | bytes 14622720 | tf_op jit(solution)/shard_map/all_gather | solution.py:96
  185.1 543.9 %all-reduce.12.cloned.1.call-start = ((), (), s32[]{:S(2)}) async-start(), calls=%async_computation.16 | async-start | bytes 6291456 | tf_op jit(solution)/shard_map/psum | solution.py:206
  270.3 107.4 %copy-start.28 = (bf16[512,1536]{1,0:T(8,128)(2,1)S(1)}, bf16[512,1536]{1,0:T(8,128)(2,1)}, u32[]{:S(2)}) copy-start(bf16[512,1536]{1,0:T(8,128)(2,1)} %fusion.58) | copy-start | bytes 4718596
  392.0 201.8 %copy-start.30 = (bf16[512,1536]{1,0:T(8,128)(2,1)S(1)}, bf16[512,1536]{1,0:T(8,128)(2,1)}, u32[]{:S(2)}) copy-start(bf16[512,1536]{1,0:T(8,128)(2,1)} %multiply_convert_fusion.1) | copy-start | bytes 4718596
  644.9 250.3 %reduce-scatter.14.cloned.1.call-start = ((), (), s32[]{:S(2)}) async-start(), calls=%async_computation.17 | async-start | bytes 4718592 | tf_op jit(solution)/shard_map/reduce_scatter | solution.py:263
  644.9 88.5 %copy-start.18 = (bf16[4,128,1536]{2,1,0:T(8,128)(2,1)S(1)}, bf16[4,128,1536]{2,1,0:T(8,128)(2,1)}, u32[]{:S(2)}) copy-start(bf16[4,128,1536]{2,1,0:T(8,128)(2,1)} %param.27) | copy-start | bytes 4718596
  806.3 170.3 %reduce-scatter.30.cloned.1.call-start = ((), (), s32[]{:S(2)}) async-start(), calls=%async_computation.25 | async-start | bytes 1114112
  824.5 71.9 %copy-start.42 = (f32[512]{0:T(512)S(1)}, f32[512]{0:T(512)}, u32[]{:S(2)}) copy-start(f32[512]{0:T(512)} %copy-done.41) | copy-start | bytes 6148
  824.5 71.9 %copy-start.53 = (f32[64]{0:T(128)S(1)}, f32[64]{0:T(128)}, u32[]{:S(2)}) copy-start(f32[64]{0:T(128)} %copy-done.52) | copy-start | bytes 772
  824.5 72.6 %copy-start.25 = (bf16[1536,128]{1,0:T(8,128)(2,1)S(1)}, bf16[1536,128]{1,0:T(8,128)(2,1)}, u32[]{:S(2)}) copy-start(bf16[1536,128]{1,0:T(8,128)(2,1)} %copy-done.24) | copy-start | bytes 1179652
  902.9 144.6 %all-reduce.14.cloned.1.call-start = ((), (), s32[]{:S(2)}) async-start(), calls=%async_computation.26 | async-start | bytes 6291456 | tf_op jit(solution)/shard_map/psum | solution.py:182
  906.7 221.4 %reduce-scatter.16.cloned.1.call-start = ((), (), s32[]{:S(2)}) async-start(), calls=%async_computation.18 | async-start | bytes 5013504 | tf_op jit(solution)/shard_map/reduce_scatter | solution.py:310
  912.0 295.3 %reduce-scatter.22.cloned.1.call-start = ((), (), s32[]{:S(2)}) async-start(), calls=%async_computation.21 | async-start | bytes 5013504 | tf_op jit(solution)/shard_map/reduce_scatter | solution.py:313
  918.7 348.5 %reduce-scatter.18.cloned.1.call-start = ((), (), s32[]{:S(2)}) async-start(), calls=%async_computation.19 | async-start | bytes 835584 | tf_op jit(solution)/shard_map/reduce_scatter | solution.py:311
  921.6 405.3 %reduce-scatter.20.cloned.1.call-start = ((), (), s32[]{:S(2)}) async-start(), calls=%async_computation.20 | async-start | bytes 835584 | tf_op jit(solution)/shard_map/reduce_scatter | solution.py:312
  924.3 671.0 %reduce-scatter.24.cloned.1.call-start = ((), (), s32[]{:S(2)}) async-start(), calls=%async_computation.22 | async-start | bytes 29245440 | tf_op jit(solution)/shard_map/reduce_scatter | solution.py:318
  939.4 924.2 %reduce-scatter.26.cloned.1.call-start = ((), (), s32[]{:S(2)}) async-start(), calls=%async_computation.23 | async-start | bytes 29245440 | tf_op jit(solution)/shard_map/reduce_scatter | solution.py:319
  957.6 1174.4 %reduce-scatter.28.cloned.1.call-start = ((), (), s32[]{:S(2)}) async-start(), calls=%async_computation.24 | async-start | bytes 29245440 | tf_op jit(solution)/shard_map/reduce_scatter | solution.py:320
  974.1 73.4 %copy-start.45 = (f32[512]{0:T(512)S(1)}, f32[512]{0:T(512)}, u32[]{:S(2)}) copy-start(f32[512]{0:T(512)} %copy-done.44) | copy-start | bytes 6148
  974.1 76.4 %copy-start.43 = (f32[1536]{0:T(1024)S(1)}, f32[1536]{0:T(1024)}, u32[]{:S(2)}) copy-start(f32[1536]{0:T(1024)} %get-tuple-element.866) | copy-start | bytes 18436
  974.2 141.6 %copy-start.6 = (f32[512,1536]{1,0:T(8,128)S(1)}, f32[512,1536]{1,0:T(8,128)}, u32[]{:S(2)}) copy-start(f32[512,1536]{1,0:T(8,128)} %copy-done.4) | copy-start | bytes 9437188
  (57 other events, 391.1 us)
Sparse Core Ops, SparseCore 0:
  10.2 46.0 all-gather.8
  87.0 48.2 all-gather.6
  137.5 40.8 all-gather.10
  183.3 84.5 all-reduce.9
  270.0 107.6 all-gather.16
  379.8 105.8 all-gather.12
  487.9 105.8 all-gather.14
  645.0 83.9 all-reduce.11
  806.5 88.6 reduce-scatter.13
  903.0 57.1 reduce-scatter.29
  962.6 84.8 all-reduce.13
  1051.8 76.2 reduce-scatter.15
  1132.5 74.7 reduce-scatter.21
  1211.3 55.8 reduce-scatter.17
  1271.2 55.7 reduce-scatter.19
  1331.5 263.6 reduce-scatter.23
  1599.8 263.7 reduce-scatter.25
  1868.2 263.7 reduce-scatter.27
where the time goes:
time: 2140 us
  waiting for transfers between devices  1630 us (76%)
  matrix products  246 us (11%)
  blocking collectives  158 us (7%)
  other arithmetic  48.2 us (2%)
  local copies, waits for them, and re-layouts  40.8 us (2%)
    reduce_scatter x1, waiting for transfers between devices, on_device(): lax.psum_scatter(down_sum, ('dp', 'seq'), scatter_dimension=1, tiled=True)  268 us
    reduce_scatter x1, waiting for transfers between devices, on_device(): lax.psum_scatter(up_sum, ('dp', 'seq'), scatter_dimension=0, tiled=True)  268 us
    reduce_scatter x1, waiting for transfers between devices, on_device(): lax.psum_scatter(gate_sum, ('dp', 'seq'), scatter_dimension=0, tiled=True)  268 us
    all_gather x1, waiting for transfers between devices, on_device(): lax.all_gather(w_down, ('dp', 'seq'), axis=1, tiled=True)  104 us
    all_gather x1, waiting for transfers between devices, on_device(): lax.all_gather(w_up, ('dp', 'seq'), axis=0, tiled=True)  95 us
    all_gather x1, waiting for transfers between devices, on_device(): lax.all_gather(w_gate, ('dp', 'seq'), axis=0, tiled=True)  93.7 us
    psum x1, waiting for transfers between devices, on_device(): lax.psum(through_weight(d_gate, full_gate) + through_weight(d_up, full_up...  82.6 us
    psum x1, waiting for transfers between devices, on_device(): middle = hidden + lax.psum(plain_dot(mixed, full_out), 'head')  79.8 us
  transfers between devices with their start and end apart: 18, of which 16 were waited for; matrix products, arithmetic and copies ran while one was open for 9% of the time, Pallas kernels for 0%

commit v1 on v0

--- a/solution.py
+++ b/solution.py
@@ -203,7 +203,13 @@
     d_up = (d_product * activated).astype(jnp.bfloat16)
     grad_gate_w = grad_of_weight(normed_two, d_gate)
     grad_up_w = grad_of_weight(normed_two, d_up)
-    back_two = lax.psum(through_weight(d_gate, full_gate) + through_weight(d_up, full_up), "head")
+
+    def convert_the_sums_all(obj, axis_tag):
+        return lax.all_gather(obj, axis_tag).sum(axis=0)
+
+    back_two = convert_the_sums_all(
+        through_weight(d_gate, full_gate) + through_weight(d_up, full_up), "head"
+    )
     gain_two_grad = jnp.sum(back_two * middle * scale_two, axis=0)
     gate_sum, up_sum, down_sum, gain_two_sum = (grad_gate_w, grad_up_w, grad_down_w, gain_two_grad)
     d_middle = cotangent + norm_back(back_two, middle, scale_two, gain_two)

time: 2140 us -> 2140 us (level)
    psum x1 -> x0, waiting for transfers between devices: 82.6 us -> none  [on_device(): lax.psum(through_weight(d_gate, full_gate) + through_weight(d_up, full_up...]
    all_gather x0 -> x1, waiting for transfers between devices: none -> 76.5 us  [convert_the_sums_all(): return lax.all_gather(obj, axis_tag).sum(axis=0)]
where the time goes in v1:
time: 2140 us; the launch traced here: 2130 us
  waiting for transfers between devices  1620 us (76%)
  matrix products  241 us (11%)
  blocking collectives  158 us (7%)
  other arithmetic  55.8 us (3%)
  local copies, waits for them, and re-layouts  37.6 us (2%)
    reduce_scatter x1, waiting for transfers between devices, on_device(): lax.psum_scatter(down_sum, ('dp', 'seq'), scatter_dimension=1, tiled=True)  268 us
    reduce_scatter x1, waiting for transfers between devices, on_device(): lax.psum_scatter(up_sum, ('dp', 'seq'), scatter_dimension=0, tiled=True)  268 us
    reduce_scatter x1, waiting for transfers between devices, on_device(): lax.psum_scatter(gate_sum, ('dp', 'seq'), scatter_dimension=0, tiled=True)  268 us
    all_gather x1, waiting for transfers between devices, on_device(): lax.all_gather(w_gate, ('dp', 'seq'), axis=0, tiled=True)  104 us
    all_gather x1, waiting for transfers between devices, on_device(): lax.all_gather(w_down, ('dp', 'seq'), axis=1, tiled=True)  94.6 us
    all_gather x1, waiting for transfers between devices, on_device(): lax.all_gather(w_up, ('dp', 'seq'), axis=0, tiled=True)  94.1 us
    psum x1, waiting for transfers between devices, on_device(): middle = hidden + lax.psum(plain_dot(mixed, full_out), 'head')  79.8 us
    reduce_scatter x1, waiting for transfers between devices, on_device(): lax.psum_scatter(grad_out_w, ('dp', 'seq'), scatter_dimension=1, tiled=True)  79.2 us
  transfers between devices with their start and end apart: 18, of which 16 were waited for; matrix products, arithmetic and copies ran while one was open for 9% of the time, Pallas kernels for 0%

profile of v1, /device:TPU:0, one launch (start us, length us, event | category | flops | bytes accessed | tf_op | source)
XLA Modules:
  0.0 2130.8 jit_solution(3628382533721101746)
XLA Ops:
  8.7 38.7 %all_gather.40 = bf16[1536,128]{1,0:T(8,128)(2,1)S(1)} all-gather(bf16[96,128]{1,0:T(8,128)(2,1)} %param.31), channel_id=1, replica_groups=mesh['dp'=2,'seq'=8,'head'=2] {'dp','seq'}, dimensions={0}, use_global_device_ids=true | all-gather | bytes 417792 | tf_op jit(solution)/shard_map/all_gather | solution.py:93
  53.7 30.5 %all_gather.41 = bf16[1536,128]{1,0:T(8,128)(2,1)S(1)} all-gather(bf16[96,128]{1,0:T(8,128)(2,1)S(1)} %copy-done.40), channel_id=1, replica_groups=mesh['dp'=2,'seq'=8,'head'=2] {'dp','seq'}, dimensions={0}, use_global_device_ids=true | all-gather | bytes 417792 | tf_op jit(solution)/shard_map/all_gather | solution.py:94
  89.3 26.5 %all_gather.43 = s32[2,4,1024]{2,1,0:T(4,128)S(1)} all-gather(s32[2,4,128]{2,1,0:T(4,128)S(1)} %pad_add_fusion), channel_id=1, replica_groups=mesh['dp'=2,'seq'=8,'head'=2] {'seq'}, dimensions={2}, use_global_device_ids=true | all-gather | bytes 36864 | tf_op jit(solution)/shard_map/all_gather | solution.py:101
  128.0 8.2 all-gather.9.cloned.1.call-done
  136.3 19.8 while.60
  156.1 10.1 while.61
  168.5 10.9 all-gather.13.cloned.1.call-done
  189.1 79.8 %all-reduce.9.cloned.1.call-done = f32[512,1536]{1,0:T(8,128)} async-done(((f32[512,1536]{1,0:T(8,128)}), f32[512,1536]{1,0:T(8,128)}) %all-reduce.9.cloned.1.call-update) | async-done | bytes 3145744 | tf_op jit(solution)/shard_map/psum | solution.py:173
  274.4 104.3 %all-gather.15.cloned.1.call-done = bf16[1536,4480]{1,0:T(8,128)(2,1)} async-done(((bf16[96,4480]{1,0:T(8,128)(2,1)}), bf16[1536,4480]{1,0:T(8,128)(2,1)}) %all-gather.15.cloned.1.call-update) | async-done | bytes 13762576 | tf_op jit(solution)/shard_map/all_gather | solution.py:95
  378.7 13.4 fusion.107
  392.1 94.6 %all-gather.19.cloned.1.call-done = bf16[4480,1536]{0,1:T(8,128)(2,1)} async-done(((bf16[4480,96]{0,1:T(8,128)(2,1)}), bf16[4480,1536]{0,1:T(8,128)(2,1)}) %all-gather.19.cloned.1.call-update) | async-done | bytes 13762576 | tf_op jit(solution)/shard_map/all_gather | solution.py:98
  486.7 14.0 convolution_convert_fusion
  500.7 94.1 %all-gather.17.cloned.1.call-done = bf16[1536,4480]{1,0:T(8,128)(2,1)} async-done(((bf16[96,4480]{1,0:T(8,128)(2,1)}), bf16[1536,4480]{1,0:T(8,128)(2,1)}) %all-gather.17.cloned.1.call-update) | async-done | bytes 13762576 | tf_op jit(solution)/shard_map/all_gather | solution.py:96
  594.8 17.1 fusion.46
  614.0 11.9 fusion.108
  625.9 19.1 convolution_add_fusion.2
  647.2 76.5 %all-gather.21.cloned.1.call-done = f32[1024,1536]{1,0:T(8,128)} async-done(((f32[512,1536]{1,0:T(8,128)}), f32[1024,1536]{1,0:T(8,128)}) %all-gather.21.cloned.1.call-update) | async-done | bytes 6291472 | tf_op jit(solution)/shard_map/all_gather | solution.py:208
  740.2 20.2 while.62
  762.9 38.9 %while.63 = (s32[]{:T(128)}, f32[4,128,6,128]{1,3,2,0:T(8,128)}, f32[4,1024,256]{1,2,0:T(8,128)}, bf16[4,1024,256]{2,1,0:T(8,128)(2,1)}, s32[4,128]{1,0:T(4,128)...) while((s32[]{:T(128)}, f32[4,128,6,128]{1,3,2,0:T(8,128)}, ...), condition=%wide.region_16.17_spmd.clone, body=%wide.region_15.16_spmd.clone.sunk | while | flops 2031091712 | bytes 71655744 | solution.py:260
  801.9 13.2 convolution_convert_fusion.1
  823.2 67.5 %reduce-scatter.14.cloned.1.call-done = f32[4,128,256]{1,2,0:T(8,128)} async-done(((f32[4,1024,256]{1,2,0:T(8,128)}), f32[4,128,256]{1,2,0:T(8,128)}) %reduce-scatter.14.cloned.1.call-update) | async-done | bytes 524304 | tf_op jit(solution)/shard_map/reduce_scatter | solution.py:269
  916.1 15.0 fusion.111
  931.2 18.1 fusion.103
  950.7 15.2 fusion.112
  969.9 68.8 %all-reduce.11.cloned.1.call-done = (bf16[512,1536]{1,0:T(8,128)(2,1)}, bf16[512,1536]{1,0:T(8,128)(2,1)}) async-done(((bf16[512,1536]{1,0:T(8,128)(2,1)}, bf16[512,1536]{1,0:T(8,128)(2,1)}), (bf16[512,1536]{1,0:T(8,128)(2,1)}, bf16[512,1536]{1,0:T(8,128)(2,1)})) %all-reduce.11.cloned.1.call-update) | async-done | bytes 3145744 | tf_op jit(solution)/shard_map/psum | solution.py:182
  1041.7 62.7 %all-reduce.4 = (f32[1536]{0:T(1024)S(1)}, f32[6,128]{1,0:T(8,128)S(1)}, f32[1,128]{1,0:T(1,128)S(1)}, f32[1536]{0:T(1024)S(1)}) all-reduce(f32[1536]{0:T(1024)S(1)} %get-tuple-element.868, f32[6,128]{1,0:T(8,128)S(1)} %get-tuple-element.948, ...), channel_id=4, replica_groups=mesh['dp'=2,'seq'=8,'head'=2] {'dp','seq'}, use_global_device_ids=true, to_apply=%region_21.22.clone | all-reduce | flops 3968 | bytes 31744
  1119.3 79.2 %reduce-scatter.22.cloned.1.call-done = f32[768,96]{0,1:T(8,128)} async-done(((f32[768,1536]{0,1:T(8,128)}), f32[768,96]{0,1:T(8,128)}) %reduce-scatter.22.cloned.1.call-update) | async-done | bytes 294928 | tf_op jit(solution)/shard_map/reduce_scatter | solution.py:319
  1198.5 60.0 %reduce-scatter.18.cloned.1.call-done = f32[96,128]{1,0:T(8,128)} async-done(((f32[1536,128]{1,0:T(8,128)}), f32[96,128]{1,0:T(8,128)}) %reduce-scatter.18.cloned.1.call-update) | async-done | bytes 49168 | tf_op jit(solution)/shard_map/reduce_scatter | solution.py:317
  1258.5 59.8 %reduce-scatter.20.cloned.1.call-done = f32[96,128]{1,0:T(8,128)} async-done(((f32[1536,128]{1,0:T(8,128)}), f32[96,128]{1,0:T(8,128)}) %reduce-scatter.20.cloned.1.call-update) | async-done | bytes 49168 | tf_op jit(solution)/shard_map/reduce_scatter | solution.py:318
  1318.3 268.3 %reduce-scatter.24.cloned.1.call-done = f32[96,4480]{1,0:T(8,128)} async-done(((f32[1536,4480]{1,0:T(8,128)}), f32[96,4480]{1,0:T(8,128)}) %reduce-scatter.24.cloned.1.call-update) | async-done | bytes 1720336 | tf_op jit(solution)/shard_map/reduce_scatter | solution.py:324
  1586.6 268.4 %reduce-scatter.26.cloned.1.call-done = f32[96,4480]{1,0:T(8,128)} async-done(((f32[1536,4480]{1,0:T(8,128)}), f32[96,4480]{1,0:T(8,128)}) %reduce-scatter.26.cloned.1.call-update) | async-done | bytes 1720336 | tf_op jit(solution)/shard_map/reduce_scatter | solution.py:325
  1855.0 268.4 %reduce-scatter.28.cloned.1.call-done = f32[4480,96]{0,1:T(8,128)} async-done(((f32[4480,1536]{0,1:T(8,128)}), f32[4480,96]{0,1:T(8,128)}) %reduce-scatter.28.cloned.1.call-update) | async-done | bytes 1720336 | tf_op jit(solution)/shard_map/reduce_scatter | solution.py:326
  (281 shorter events, 209.2 us)
Async XLA Ops:
  7.2 43.4 %copy-start.5 = (bf16[4,128,1536]{2,1,0:T(8,128)(2,1)S(1)}, bf16[4,128,1536]{2,1,0:T(8,128)(2,1)}, u32[]{:S(2)}) copy-start(bf16[4,128,1536]{2,1,0:T(8,128)(2,1)} %param.24) | copy-start | bytes 4718596
  7.2 108.6 %all-gather.11.cloned.1.call-start = ((), (), s32[]{:S(2)}) async-start(), calls=%async_computation.10 | async-start | bytes 2506752 | tf_op jit(solution)/shard_map/all_gather | solution.py:92
  7.9 128.3 %all-gather.9.cloned.1.call-start = ((), (), s32[]{:S(2)}) async-start(), calls=%async_computation.9 | async-start | bytes 2359296 | tf_op jit(solution)/shard_map/all_gather | solution.py:123
  8.7 44.2 %copy-start.33 = (f32[1536]{0:T(1024)}, f32[1536]{0:T(1024)S(1)}, u32[]{:S(2)}) copy-start(f32[1536]{0:T(1024)S(1)} %convert_element_type.175) | copy-start | bytes 18436
  8.7 80.0 %copy-start.46 = (f32[64]{0:T(128)}, f32[64]{0:T(128)S(1)}, u32[]{:S(2)}) copy-start(f32[64]{0:T(128)S(1)} %multiply_power_fusion) | copy-start | bytes 772
  52.2 37.1 %copy-start.49 = (bf16[6,128]{1,0:T(8,128)(2,1)S(1)}, bf16[6,128]{1,0:T(8,128)(2,1)}, u32[]{:S(2)}) copy-start(bf16[6,128]{1,0:T(8,128)(2,1)} %param.30) | copy-start | bytes 4612
  52.2 37.1 %copy-start.31 = (s32[4,128]{1,0:T(4,128)S(1)}, s32[4,128]{1,0:T(4,128)}, u32[]{:S(2)}) copy-start(s32[4,128]{1,0:T(4,128)} %param.25) | copy-start | bytes 6148
  52.9 67.6 %copy-start.35 = (f32[512]{0:T(512)}, f32[512]{0:T(512)S(1)}, u32[]{:S(2)}) copy-start(f32[512]{0:T(512)S(1)} %convert_bitcast_fusion.1) | copy-start | bytes 6148
  87.8 91.5 %all-gather.13.cloned.1.call-start = ((), (), s32[]{:S(2)}) async-start(), calls=%async_computation.11 | async-start | bytes 2506752 | tf_op jit(solution)/shard_map/all_gather | solution.py:97
  88.6 180.3 %all-reduce.9.cloned.1.call-start = ((), (), s32[]{:S(2)}) async-start(), calls=%async_computation.12 | async-start | bytes 6291456 | tf_op jit(solution)/shard_map/psum | solution.py:173
  89.2 34.3 %copy-start.26 = (f32[512,64]{0,1:T(8,128)}, f32[512,64]{0,1:T(8,128)S(1)}, u32[]{:S(2)}) copy-start(f32[512,64]{0,1:T(8,128)S(1)} %get-tuple-element.976) | copy-start | bytes 393220
  184.2 194.5 %all-gather.15.cloned.1.call-start = ((), (), s32[]{:S(2)}) async-start(), calls=%async_computation.13 | async-start | bytes 14622720 | tf_op jit(solution)/shard_map/all_gather | solution.py:95
  184.8 301.9 %all-gather.19.cloned.1.call-start = ((), (), s32[]{:S(2)}) async-start(), calls=%async_computation.15 | async-start | bytes 14622720 | tf_op jit(solution)/shard_map/all_gather | solution.py:98
  185.4 409.4 %all-gather.17.cloned.1.call-start = ((), (), s32[]{:S(2)}) async-start(), calls=%async_computation.14 | async-start | bytes 14622720 | tf_op jit(solution)/shard_map/all_gather | solution.py:96
  186.1 537.6 %all-gather.21.cloned.1.call-start = ((), (), s32[]{:S(2)}) async-start(), calls=%async_computation.24 | async-start | bytes 9437184 | tf_op jit(solution)/shard_map/all_gather | solution.py:208
  274.4 212.3 %copy-start.23 = (bf16[512,1536]{1,0:T(8,128)(2,1)S(1)}, bf16[512,1536]{1,0:T(8,128)(2,1)}, u32[]{:S(2)}) copy-start(bf16[512,1536]{1,0:T(8,128)(2,1)} %fusion.58) | copy-start | bytes 4718596
  645.0 245.7 %reduce-scatter.14.cloned.1.call-start = ((), (), s32[]{:S(2)}) async-start(), calls=%async_computation.16 | async-start | bytes 4718592 | tf_op jit(solution)/shard_map/reduce_scatter | solution.py:269
  801.9 166.6 %reduce-scatter.30.cloned.1.call-start = ((), (), s32[]{:S(2)}) async-start(), calls=%async_computation.25 | async-start | bytes 1114112
  820.0 71.9 %copy-start.36 = (f32[512]{0:T(512)S(1)}, f32[512]{0:T(512)}, u32[]{:S(2)}) copy-start(f32[512]{0:T(512)} %copy-done.35) | copy-start | bytes 6148
  820.0 71.9 %copy-start.47 = (f32[64]{0:T(128)S(1)}, f32[64]{0:T(128)}, u32[]{:S(2)}) copy-start(f32[64]{0:T(128)} %copy-done.46) | copy-start | bytes 772
  823.2 70.9 %copy-start.20 = (bf16[1536,128]{1,0:T(8,128)(2,1)S(1)}, bf16[1536,128]{1,0:T(8,128)(2,1)}, u32[]{:S(2)}) copy-start(bf16[1536,128]{1,0:T(8,128)(2,1)} %copy-done.19) | copy-start | bytes 1179652
  894.1 144.6 %all-reduce.11.cloned.1.call-start = ((), (), s32[]{:S(2)}) async-start(), calls=%async_computation.26 | async-start | bytes 6291456 | tf_op jit(solution)/shard_map/psum | solution.py:182
  898.5 220.8 %reduce-scatter.16.cloned.1.call-start = ((), (), s32[]{:S(2)}) async-start(), calls=%async_computation.17 | async-start | bytes 5013504 | tf_op jit(solution)/shard_map/reduce_scatter | solution.py:316
  903.8 294.7 %reduce-scatter.22.cloned.1.call-start = ((), (), s32[]{:S(2)}) async-start(), calls=%async_computation.20 | async-start | bytes 5013504 | tf_op jit(solution)/shard_map/reduce_scatter | solution.py:319
  910.4 348.1 %reduce-scatter.18.cloned.1.call-start = ((), (), s32[]{:S(2)}) async-start(), calls=%async_computation.18 | async-start | bytes 835584 | tf_op jit(solution)/shard_map/reduce_scatter | solution.py:317
  913.4 404.9 %reduce-scatter.20.cloned.1.call-start = ((), (), s32[]{:S(2)}) async-start(), calls=%async_computation.19 | async-start | bytes 835584 | tf_op jit(solution)/shard_map/reduce_scatter | solution.py:318
  916.0 670.6 %reduce-scatter.24.cloned.1.call-start = ((), (), s32[]{:S(2)}) async-start(), calls=%async_computation.21 | async-start | bytes 29245440 | tf_op jit(solution)/shard_map/reduce_scatter | solution.py:324
  931.1 923.9 %reduce-scatter.26.cloned.1.call-start = ((), (), s32[]{:S(2)}) async-start(), calls=%async_computation.22 | async-start | bytes 29245440 | tf_op jit(solution)/shard_map/reduce_scatter | solution.py:325
  949.3 1174.2 %reduce-scatter.28.cloned.1.call-start = ((), (), s32[]{:S(2)}) async-start(), calls=%async_computation.23 | async-start | bytes 29245440 | tf_op jit(solution)/shard_map/reduce_scatter | solution.py:326
  965.9 72.8 %copy-start.39 = (f32[512]{0:T(512)S(1)}, f32[512]{0:T(512)}, u32[]{:S(2)}) copy-start(f32[512]{0:T(512)} %copy-done.38) | copy-start | bytes 6148
  965.9 75.8 %copy-start.37 = (f32[1536]{0:T(1024)S(1)}, f32[1536]{0:T(1024)}, u32[]{:S(2)}) copy-start(f32[1536]{0:T(1024)} %get-tuple-element.866) | copy-start | bytes 18436
  965.9 141.0 %copy-start.4 = (f32[512,1536]{1,0:T(8,128)S(1)}, f32[512,1536]{1,0:T(8,128)}, u32[]{:S(2)}) copy-start(f32[512,1536]{1,0:T(8,128)} %copy-done.2) | copy-start | bytes 9437188
  (43 other events, 232.7 us)
Sparse Core Ops, SparseCore 0:
  10.2 45.8 all-gather.10
  88.0 48.2 all-gather.8
  138.5 40.8 all-gather.12
  184.3 84.5 all-reduce.8
  271.0 107.6 all-gather.14
  380.8 105.8 all-gather.18
  488.9 105.8 all-gather.16
  645.2 78.5 all-gather.20
  802.0 88.6 reduce-scatter.13
  894.2 57.3 reduce-scatter.29
  953.9 84.7 all-reduce.10
  1043.0 76.2 reduce-scatter.15
  1123.7 74.7 reduce-scatter.21
  1202.5 55.9 reduce-scatter.17
  1262.5 55.7 reduce-scatter.19
  1322.8 263.7 reduce-scatter.23
  1591.1 263.8 reduce-scatter.25
  1859.6 263.8 reduce-scatter.27
